TPU v7x, 256 devices: a whole 4x4x8 slice. The times are simulated.
256 devices in a mesh: mem: 32 (over z_hi, y, core), lat: 8 (over z_lo, x).
Axes of the slice: x: 4, y: 4, z: 8 (z_hi: 4, z_lo: 2; z = z_hi * 2 + z_lo), core: 2. Of those that a mesh axis runs over, the one named last changes fastest.
Arguments:
- controls: bfloat16 [128, 64, 256, 256], P('mem', None, 'lat'), may hold values from -6 to 6
- spread: bfloat16 [128, 64, 256, 256], P('mem', None, 'lat'), may hold values from -1.5 to 1.5
- classes: int32 [256, 256], P('lat'), may hold values from 0 to 7
- prec_table: float32 [8, 64], replicated, may hold values from 0.25 to 4
- vert_loc: bfloat16 [64, 64], replicated, may hold values from 0 to 1
- lon_loc: bfloat16 [256, 256], replicated, may hold values from 0 to 1
- lat_loc: bfloat16 [256, 256], replicated, may hold values from 0 to 1
Outputs:
- localized: bfloat16 [128, 64, 256, 256], P('mem', None, 'lat')
All inputs are finite; a program needn't handle non-finite values.
Results may differ from a plain program's by a relative error of at most 0.0064.
Values may be sent and summed in bfloat16 or wider, within the bound.
No kernel may reach another device: no remote copies, remote signals or barrier semaphores. Data moves between devices by JAX's collectives and lax.ppermute only.
A program may use at most 128 MiB of HBM per device.

v0:
```python
import jax
import jax.numpy as jnp
from jax import lax
from jax.sharding import Mesh
from jax.sharding import PartitionSpec as P

MEM = ("mem_0", "mem_1", "mem_2")


def split_up(shard, dim, peers):
    lengths = shard.shape
    parts = shard.reshape(*lengths[:dim], peers, lengths[dim] // peers, *lengths[dim + 1 :])
    return jnp.moveaxis(parts, dim, 0)


def sent_and_summed(shard, axis, dim):
    parts = split_up(shard, dim, lax.axis_size(axis))
    arrived = lax.all_to_all(parts, axis, split_axis=0, concat_axis=0, tiled=True)
    return arrived.sum(axis=0)


def sum_by_axis(shard, axes, dim):
    far, near = axes
    own = sent_and_summed(split_up(shard, dim, lax.axis_size(far)), near, dim + 1)
    return jnp.sum(lax.all_to_all(own, far, 0, 0, tiled=True), axis=0)


def padded_to(lines, peers):
    spare = -len(lines) % peers
    return jnp.pad(lines, [(0, spare)] + [(0, 0)] * (lines.ndim - 1))


def copy_for_each(shard, axis):
    copies = jnp.broadcast_to(shard, (lax.axis_size(axis), *shard.shape))
    return lax.all_to_all(copies, axis, split_axis=0, concat_axis=0, tiled=True)


def joined_along(parts, dim):
    parts = jnp.moveaxis(parts, 0, dim)
    lengths = parts.shape
    return parts.reshape(*lengths[:dim], lengths[dim] * lengths[dim + 1], *lengths[dim + 2 :])


def gathered_by_axis(shard, axes, dim):
    far, near = axes
    parts = copy_for_each(copy_for_each(shard, far), near)
    return joined_along(parts.swapaxes(0, 1).reshape(-1, *shard.shape), dim)


def sum_by_parts(shard, axes):
    lines = shard.reshape(-1, shard.shape[-1])
    own = sum_by_axis(padded_to(lines, lax.axis_size(axes[0]) * lax.axis_size(axes[1])), axes, 0)
    whole = gathered_by_axis(own, axes, 0)
    return whole[: len(lines)].reshape(shard.shape)


def lookup(table, classes):
    numbers = jnp.arange(table.shape[0], dtype=jnp.int32)
    onehot = (classes[None, :, :] == numbers[:, None, None]).astype(jnp.float32)
    return jnp.einsum("kl,kab->lab", table, onehot, precision=lax.Precision.HIGHEST)


def local(controls, spread, classes, prec_table, vert_loc, lon_loc, lat_loc):
    partial_value = jnp.sum(spread.astype(jnp.float32) * controls.astype(jnp.float32), axis=0)
    summed = sum_by_parts(partial_value, (("mem_0", "mem_1"), "mem_2"))
    weighted = summed * lookup(prec_table, classes)
    adjoint = (spread.astype(jnp.float32) * weighted[None]).astype(jnp.bfloat16)
    along_lon = jnp.einsum(
        "mlac,bc->mlab", adjoint, lon_loc, preferred_element_type=jnp.float32
    ).astype(jnp.bfloat16)
    sending = jnp.einsum(
        "lj,mjab->mlab", vert_loc, along_lon, preferred_element_type=jnp.float32
    ).astype(jnp.bfloat16)
    return jnp.einsum(
        "ac,mlcb->mlba",
        lat_loc,
        lax.all_to_all(sending, "lat", split_axis=3, concat_axis=2, tiled=True),
        preferred_element_type=jnp.float32,
    ).astype(jnp.bfloat16)


def solution(mesh):
    finer = Mesh(
        mesh.devices.reshape(4, 4, 2, mesh.shape["lat"]), ("mem_0", "mem_1", "mem_2", "lat")
    )
    placed = (
        P(MEM, None, "lat", None),
        P(MEM, None, "lat", None),
        P("lat", None),
        P(),
        P(),
        P(),
        P(),
    )
    return jax.shard_map(
        local, mesh=finer, in_specs=placed, out_specs=P(MEM, None, "lat", None), check_vma=False
    )
```

profile of v0, /device:TPU:1, one launch (start us, length us, event | category | flops | bytes accessed | tf_op | source)
XLA Modules:
  0.0 227.9 jit_solution(4709802452765705456)
XLA Ops:
  0.0 0.0 copy-start
  0.0 5.7 %fusion = f32[64,32,256]{2,1,0:T(8,128)S(1)} fusion(bf16[4,64,32,256]{3,2,1,0:T(8,128)(2,1)} %param.8, bf16[4,64,32,256]{3,2,1,0:T(8,128)(2,1)} %param.7), kind=kLoop, calls=%fused_computation.2 | loop fusion | flops 7864320 | bytes 10485760 | tf_op jit(solution)/shard_map/reduce_sum | solution.py:64
  5.7 0.1 copy.27
  5.8 8.2 %all_to_all.38 = f32[2,16,64,256]{3,2,1,0:T(8,128)S(1)} all-to-all(f32[2,16,64,256]{3,2,1,0:T(8,128)S(1)} %copy.27), channel_id=1, replica_groups=mesh['mem_0'=4,'mem_1'=4,'mem_2'=2,'lat'=8] {'mem_2'}, dimensions={0} | all-to-all | bytes 4194304 | tf_op jit(solution)/shard_map/all_to_all | solution.py:18
  14.1 0.2 reduce_sum.28
  14.3 34.9 %all_to_all.39 = f32[16,64,256]{2,1,0:T(8,128)S(1)} all-to-all(f32[16,64,256]{2,1,0:T(8,128)S(1)} %reduce_sum.28), channel_id=1, replica_groups=mesh['mem_0'=4,'mem_1'=4,'mem_2'=2,'lat'=8] {'mem_0','mem_1'}, dimensions={0} | all-to-all | bytes 2097152 | tf_op jit(solution)/shard_map/all_to_all | solution.py:25
  49.3 0.1 reduce_sum.29
  49.3 0.1 broadcast_in_dim.4
  49.4 35.8 %all_to_all.40 = f32[16,64,256]{2,1,0:T(8,128)S(1)} all-to-all(f32[16,64,256]{2,1,0:T(8,128)S(1)} %broadcast_in_dim.4), channel_id=1, replica_groups=mesh['mem_0'=4,'mem_1'=4,'mem_2'=2,'lat'=8] {'mem_0','mem_1'}, dimensions={0} | all-to-all | bytes 2097152 | tf_op jit(solution)/shard_map/all_to_all | solution.py:35
  85.2 0.3 broadcast_in_dim.10
  85.5 0.0 copy-start.4
  85.5 0.0 copy-start.6
  85.5 6.3 %all_to_all.41 = f32[2,16,64,256]{3,2,1,0:T(8,128)S(1)} all-to-all(f32[2,16,64,256]{3,2,1,0:T(8,128)S(1)} %broadcast_in_dim.10), channel_id=1, replica_groups=mesh['mem_0'=4,'mem_1'=4,'mem_2'=2,'lat'=8] {'mem_2'}, dimensions={0} | all-to-all | bytes 4194304 | tf_op jit(solution)/shard_map/all_to_all | solution.py:35
  91.8 0.2 copy.28
  92.0 0.0 copy-done.4
  92.0 0.0 copy-done.6
  92.0 0.0 copy-start.2
  92.1 2.1 bitcast_multiply_fusion
  94.2 1.2 copy.30
  95.4 0.0 copy-done.2
  95.4 0.0 copy-start.5
  95.4 3.4 %fusion.1 = bf16[4,64,32,256]{3,2,1,0:T(8,128)(2,1)} fusion(bf16[4,64,32,256]{3,2,1,0:T(8,128)(2,1)S(1)} %copy-done.2, f32[64,32,256]{2,1,0:T(8,128)S(1)} %copy.30), kind=kLoop, calls=%fused_computation.3 | loop fusion | flops 6291456 | bytes 10485760 | tf_op jit(solution)/shard_map/convert_element_type | solution.py:67
  98.8 0.0 copy-done
  98.8 0.0 copy-done.5
  98.8 7.3 %convert_bitcast_fusion = bf16[4,64,32,256]{3,1,2,0:T(8,128)(2,1)} fusion(bf16[4,64,32,256]{3,2,1,0:T(8,128)(2,1)} %fusion.1, bf16[256,256]{1,0:T(8,128)(2,1)S(1)} %copy-done, bf16[64,64]{1,0:T(8,128)(2,1)S(1)} %copy-done.5), kind=kOutput, calls=%fused_computation.6 | convolution fusion | flops 1346371584 | bytes 8527872 | tf_op jit(solution)/shard_map/lj,mjab->mlab/dot_general | solution.py:71
  106.1 13.0 %copy.32 = bf16[4,64,32,256]{1,2,0,3:T(8,128)(2,1)} copy(bf16[4,64,32,256]{3,1,2,0:T(8,128)(2,1)} %convert_bitcast_fusion) | data formatting | bytes 8388608 | tf_op jit(solution)/shard_map/convert_element_type | solution.py:73
  119.0 10.5 %reshape.8 = bf16[8,2,131072]{2,1,0:T(2,128)(2,1)} reshape(bf16[256,4,32,64]{3,2,1,0:T(8,128)(2,1)} %bitcast.36) | data formatting | bytes 8388608
  129.5 52.7 %all_to_all.42 = bf16[8,2,131072]{2,1,0:T(2,128)(2,1)} all-to-all(bf16[8,2,131072]{2,1,0:T(2,128)(2,1)} %reshape.8), channel_id=1, replica_groups=mesh['mem_0'=4,'mem_1'=4,'mem_2'=2,'lat'=8] {'lat'}, dimensions={0} | all-to-all | bytes 8388608 | tf_op jit(solution)/shard_map/all_to_all | solution.py:77
  182.2 10.3 %reshape.9 = bf16[256,4,32,64]{3,2,1,0:T(8,128)(2,1)} reshape(bf16[8,2,131072]{2,1,0:T(2,128)(2,1)} %all_to_all.42) | data formatting | bytes 8388608
  192.5 16.3 %copy.34 = bf16[4,64,8,32,32]{1,4,3,2,0:T(8,128)(2,1)} copy(bf16[4,64,8,32,32]{1,3,0,4,2:T(8,128)(2,1)} %bitcast.37) | data formatting | bytes 8388608 | tf_op jit(solution)/shard_map/all_to_all | solution.py:77
  208.8 0.0 copy-start.3
  208.8 0.0 copy-start.1
  208.8 13.5 %copy.35 = bf16[4,64,256,32]{2,3,1,0:T(8,128)(2,1)} copy(bf16[4,64,256,32]{1,3,2,0:T(8,128)(2,1)} %bitcast.38) | data formatting | bytes 8388608 | tf_op jit(solution)/shard_map/all_to_all | solution.py:77
  222.4 0.0 copy-done.3
  222.4 5.5 %convolution_convert_fusion = bf16[4,64,32,256]{3,2,1,0:T(8,128)(2,1)} fusion(bf16[4,64,256,32]{2,3,1,0:T(8,128)(2,1)} %copy.35, bf16[256,256]{1,0:T(8,128)(2,1)S(1)} %copy-done.3), kind=kOutput, calls=%fused_computation.9 | convolution fusion | flops 1075838976 | bytes 8519680 | tf_op jit(solution)/shard_map/ac,mlcb->mlba/dot_general | solution.py:74
  227.9 0.0 copy-done.1
Async XLA Ops:
  0.0 98.8 %copy-start = (bf16[256,256]{1,0:T(8,128)(2,1)S(1)}, bf16[256,256]{1,0:T(8,128)(2,1)}, u32[]{:S(2)}) copy-start(bf16[256,256]{1,0:T(8,128)(2,1)} %param.12) | copy-start | bytes 393220
  85.5 6.5 %copy-start.4 = (s32[32,256]{1,0:T(8,128)S(1)}, s32[32,256]{1,0:T(8,128)}, u32[]{:S(2)}) copy-start(s32[32,256]{1,0:T(8,128)} %param.9) | copy-start | bytes 98308
  85.5 6.5 %copy-start.6 = (f32[8,64]{1,0:T(8,128)S(1)}, f32[8,64]{1,0:T(8,128)}, u32[]{:S(2)}) copy-start(f32[8,64]{1,0:T(8,128)} %param.10) | copy-start | bytes 6148
  92.0 3.4 %copy-start.2 = (bf16[4,64,32,256]{3,2,1,0:T(8,128)(2,1)S(1)}, bf16[4,64,32,256]{3,2,1,0:T(8,128)(2,1)}, u32[]{:S(2)}) copy-start(bf16[4,64,32,256]{3,2,1,0:T(8,128)(2,1)} %param.8) | copy-start | bytes 12582916
  95.4 3.4 %copy-start.5 = (bf16[64,64]{1,0:T(8,128)(2,1)S(1)}, bf16[64,64]{1,0:T(8,128)(2,1)}, u32[]{:S(2)}) copy-start(bf16[64,64]{1,0:T(8,128)(2,1)} %param.11) | copy-start | bytes 24580
  208.8 13.5 %copy-start.3 = (bf16[256,256]{1,0:T(8,128)(2,1)S(1)}, bf16[256,256]{1,0:T(8,128)(2,1)}, u32[]{:S(2)}) copy-start(bf16[256,256]{1,0:T(8,128)(2,1)} %param.13) | copy-start | bytes 393220
  208.8 19.0 %copy-start.1 = (bf16[256,256]{1,0:T(8,128)(2,1)S(1)}, bf16[256,256]{1,0:T(8,128)(2,1)}, u32[]{:S(2)}) copy-start(bf16[256,256]{1,0:T(8,128)(2,1)} %param.12) | copy-start | bytes 393220
where the time goes:
time: 229 us; the launch traced here: 228 us
  blocking collectives  138 us (60%)
  local copies, waits for them, and re-layouts  65.5 us (29%)
  matrix products  14.9 us (7%)
  other arithmetic  9.34 us (4%)
    all_to_all x1, blocking collectives, local(): lax.all_to_all(sending, 'lat', split_axis=3, concat_axis=2, tiled=True)  52.7 us
    all_to_all x2, blocking collectives, copy_for_each(): return lax.all_to_all(copies, axis, split_axis=0, concat_axis=0, tiled=True)  42.1 us
    all_to_all x1, blocking collectives, sum_by_axis(): return jnp.sum(lax.all_to_all(own, far, 0, 0, tiled=True), axis=0)  34.9 us
    all_to_all x2, local copies, waits for them, and re-layouts, local(): lax.all_to_all(sending, 'lat', split_axis=3, concat_axis=2, tiled=True)  29.8 us
    unnamed x16, local copies, waits for them, and re-layouts  20.8 us
    convert_element_type x1, local copies, waits for them, and re-layouts, local(): sending = jnp.einsum('lj,mjab->mlab', vert_loc, along_lon, preferred_elem...  13 us
    all_to_all x1, blocking collectives, sent_and_summed(): lax.all_to_all(parts, axis, split_axis=0, concat_axis=0, tiled=True)  8.25 us
    dot_general x1, matrix products, local(): jnp.einsum('lj,mjab->mlab', vert_loc, along_lon, preferred_element_type=j...  7.3 us

commit v1 on v0

v1 whole, which is shorter than its diff:
```python
import functools

import jax
import jax.numpy as jnp
from jax import lax
from jax.experimental import pallas as pl
from jax.experimental.pallas import tpu as pltpu
from jax.sharding import Mesh
from jax.sharding import PartitionSpec as P

F32 = jnp.float32
BF16 = jnp.bfloat16
ZH, Y, CORE = 4, 4, 2
LATS = 8
RING = ("zh", "y")
LAT = "lat"
EACH = 4


def nt_dot(a, b):
    return lax.dot_general(a, b, (((1,), (1,)), ((), ())), preferred_element_type=F32)


def compiler_params(mib):
    return pltpu.CompilerParams(
        dimension_semantics=("arbitrary",), vmem_limit_bytes=mib * 1024 * 1024
    )


def half_sum_kernel(start_ref, spread_ref, controls_ref, *rest):
    out_ref = rest[-1]
    total = spread_ref[0].astype(F32) * controls_ref[0].astype(F32)
    for k in range(1, spread_ref.shape[0]):
        total += spread_ref[k].astype(F32) * controls_ref[k].astype(F32)
    if len(rest) == 2:
        total += rest[0][...].astype(F32)
    out_ref[...] = total.astype(BF16)


def half_sum(spread, controls, half, arrived=None):
    members, levels, rows, cols = spread.shape
    step = 8
    count = levels // 2 // step
    field = pl.BlockSpec((members, step, rows, cols), lambda i, s: (0, s[0] * count + i, 0, 0))
    piece = pl.BlockSpec((step, rows, cols), lambda i, s: (i, 0, 0))
    args = (spread, controls) if arrived is None else (spread, controls, arrived)
    return pl.pallas_call(
        half_sum_kernel,
        grid_spec=pltpu.PrefetchScalarGridSpec(
            num_scalar_prefetch=1,
            grid=(count,),
            in_specs=[field, field] + [piece] * (len(args) - 2),
            out_specs=piece,
        ),
        out_shape=jax.ShapeDtypeStruct((levels // 2, rows, cols), BF16),
        compiler_params=compiler_params(8),
        name="half_sum",
    )(half, *args)


def tables_kernel(me_ref, vert_ref, lat_ref, big_ref, turned_ref):
    levels = vert_ref.shape[0]
    size = levels * 8
    row = lax.broadcasted_iota(jnp.int32, (size, levels), 0) >> 3
    col = lax.broadcasted_iota(jnp.int32, (size, levels), 1)
    source = (row & ~3) | ((row + 8 - me_ref[0]) & 3)
    pick_out = jnp.where(source == col, 1.0, 0.0).astype(BF16)
    pick_in = jnp.where(row == col, 1.0, 0.0).astype(BF16)
    tall = jnp.dot(pick_out, vert_ref[...], preferred_element_type=F32).astype(BF16)
    wide = nt_dot(tall, pick_in)
    r = lax.broadcasted_iota(jnp.int32, (size, size), 0) & 7
    c = lax.broadcasted_iota(jnp.int32, (size, size), 1) & 7
    big_ref[...] = jnp.where(r == c, wide, 0.0).astype(BF16)
    for part in range(2):
        block = lat_ref[:, 128 * part : 128 * part + 128].astype(F32)
        for turn in range(EACH):
            moved = block if turn == 0 else pltpu.roll(block, 32 * turn, 1)
            turned_ref[turn, :, 128 * part : 128 * part + 128] = moved.astype(BF16)


def tables(me, vert_loc, lat_loc):
    levels = vert_loc.shape[0]
    size = lat_loc.shape[0]
    return pl.pallas_call(
        tables_kernel,
        in_specs=[
            pl.BlockSpec(memory_space=pltpu.SMEM),
            pl.BlockSpec(memory_space=pltpu.VMEM),
            pl.BlockSpec(memory_space=pltpu.VMEM),
        ],
        out_specs=[pl.BlockSpec(memory_space=pltpu.VMEM)] * 2,
        out_shape=[
            jax.ShapeDtypeStruct((levels * 8, levels * 8), BF16),
            jax.ShapeDtypeStruct((EACH, size, size), BF16),
        ],
        compiler_params=pltpu.CompilerParams(vmem_limit_bytes=16 * 1024 * 1024),
        name="tables",
    )(me, vert_loc, lat_loc)


def spread_out_kernel(half_ref, spread_ref, own_ref, other_ref, big_ref, lon_ref, out_ref, adj, mixed):
    levels, rows, cols = adj.shape
    half = levels // 2
    for which, piece in ((0, own_ref), (1, other_ref)):
        base = (half_ref[0] ^ which) * half

        @pl.loop(0, half)
        def _(i):
            adj[base + i] = spread_ref[0, base + i].astype(F32) * piece[i].astype(F32)

    for g in range(rows // 8):
        x = adj[:, 8 * g : 8 * g + 8, :].reshape(levels * 8, cols).astype(BF16)
        y = jnp.dot(big_ref[...], x, preferred_element_type=F32)
        mixed[:, 8 * g : 8 * g + 8, :] = y.reshape(levels, 8, cols)
    for n in range(levels * rows // 256):
        at = 256 // rows
        x = mixed[at * n : at * n + at].reshape(256, cols).astype(BF16)
        y = nt_dot(lon_ref[...], x).astype(BF16)
        out_ref[:, 0, :, 256 * n : 256 * n + 256] = y.reshape(LATS, cols // LATS, 256)


def spread_out(half, spread, own, other, big, lon_loc):
    members, levels, rows, cols = spread.shape
    share = cols // LATS

    def whole(x):
        return pl.BlockSpec(x.shape, lambda k, s: (0,) * x.ndim)

    return pl.pallas_call(
        spread_out_kernel,
        grid_spec=pltpu.PrefetchScalarGridSpec(
            num_scalar_prefetch=1,
            grid=(members,),
            in_specs=[
                pl.BlockSpec((1, levels, rows, cols), lambda k, s: (k, 0, 0, 0)),
                whole(own),
                whole(other),
                whole(big),
                whole(lon_loc),
            ],
            out_specs=pl.BlockSpec((LATS, 1, share, levels * rows), lambda k, s: (0, k, 0, 0)),
            scratch_shapes=[pltpu.VMEM((levels, rows, cols), F32)] * 2,
        ),
        out_shape=jax.ShapeDtypeStruct((LATS, members, share, levels * rows), BF16),
        compiler_params=compiler_params(24),
        name="spread_out",
    )(half, spread, own, other, big, lon_loc)


def finish_kernel(parts_ref, turned_ref, out_ref):
    share = parts_ref.shape[2]
    groups = parts_ref.shape[3] // 128
    lane = lax.broadcasted_iota(jnp.int32, (share, 128), 1) >> 5
    at = [lane == q for q in range(3)]
    for turn in range(EACH):
        lines = []
        for g in range(groups):
            sides = []
            for part in range(2):
                tiles = [
                    parts_ref[EACH * part + (q - turn) % EACH, 0, :, 128 * g : 128 * g + 128]
                    for q in range(EACH)
                ]
                side = tiles[3]
                for q in range(3):
                    side = jnp.where(at[q], tiles[q], side)
                sides.append(side)
            lines.append(jnp.concatenate(sides, axis=1))
        x = jnp.concatenate(lines, axis=0)
        y = nt_dot(x, turned_ref[turn]).astype(BF16)
        for g in range(groups):
            out_ref[0, EACH * g + turn] = y[share * g : share * g + share]


def finish(parts, turned):
    _, members, share, wide = parts.shape
    size = turned.shape[1]
    levels = wide // 32
    return pl.pallas_call(
        finish_kernel,
        grid=(members,),
        in_specs=[
            pl.BlockSpec((LATS, 1, share, wide), lambda k: (0, k, 0, 0)),
            pl.BlockSpec(turned.shape, lambda k: (0, 0, 0)),
        ],
        out_specs=pl.BlockSpec((1, levels, share, size), lambda k: (k, 0, 0, 0)),
        out_shape=jax.ShapeDtypeStruct((members, levels, share, size), BF16),
        compiler_params=compiler_params(16),
        name="finish",
    )(parts, turned)


def weigh_kernel(first_ref, pieces_ref, classes_ref, table_ref, out_ref):
    peers, each = pieces_ref.shape[:2]
    classes = classes_ref[...]
    for l in range(each):
        total = pieces_ref[0, l].astype(F32)
        for n in range(1, peers):
            total += pieces_ref[n, l].astype(F32)
        precision = jnp.full(classes.shape, table_ref[0, first_ref[0] + l], F32)
        for n in range(1, table_ref.shape[0]):
            precision = jnp.where(classes == n, table_ref[n, first_ref[0] + l], precision)
        weighted = (total * precision).astype(BF16)
        for n in range(peers):
            out_ref[n, l] = weighted


def weigh(first, pieces, classes, prec_table):
    vmem = pl.BlockSpec(memory_space=pltpu.VMEM)
    smem = pl.BlockSpec(memory_space=pltpu.SMEM)
    return pl.pallas_call(
        weigh_kernel,
        in_specs=[smem, vmem, vmem, smem],
        out_specs=vmem,
        out_shape=jax.ShapeDtypeStruct(pieces.shape, BF16),
        compiler_params=pltpu.CompilerParams(vmem_limit_bytes=8 * 1024 * 1024),
        name="weigh",
    )(first, pieces, classes, prec_table)


def local(controls, spread, classes, prec_table, vert_loc, lon_loc, lat_loc):
    levels = spread.shape[1]
    controls = pltpu.with_memory_space_constraint(controls, pltpu.HBM)
    spread = pltpu.with_memory_space_constraint(spread, pltpu.HBM)
    core = lax.axis_index("core")
    own_half = core.reshape(1)
    other_half = (1 - core).reshape(1)
    me = lax.axis_index(LAT).reshape(1)
    swap = [(0, 1), (1, 0)]

    big, turned = tables(me, vert_loc, lat_loc)
    arrived = lax.ppermute(half_sum(spread, controls, other_half), "core", swap)
    chip = half_sum(spread, controls, own_half, arrived)
    peers = ZH * Y
    each = levels // (CORE * peers)
    pieces = lax.all_to_all(
        chip.reshape(peers, each, *chip.shape[1:]), RING, split_axis=0, concat_axis=0, tiled=True
    )
    first = ((core * peers + lax.axis_index(RING)) * each).reshape(1)
    copies = weigh(first, pieces, classes, prec_table)
    own = lax.all_to_all(copies, RING, split_axis=0, concat_axis=0, tiled=True).reshape(chip.shape)
    other = lax.ppermute(own, "core", swap)
    sending = spread_out(own_half, spread, own, other, big, lon_loc)
    parts = lax.all_to_all(sending, LAT, split_axis=0, concat_axis=0, tiled=True)
    return finish(parts, turned)


def solution(mesh):
    finer = Mesh(
        mesh.devices.reshape(ZH, Y, CORE, mesh.shape["lat"]), ("zh", "y", "core", LAT)
    )
    members = P(("zh", "y", "core"), None, LAT, None)
    return jax.shard_map(
        local,
        mesh=finer,
        in_specs=(members, members, P(LAT, None), P(), P(), P(), P()),
        out_specs=members,
        check_vma=False,
    )
```

time: 229 us -> 128 us (0.56)
  local copies, waits for them, and re-layouts: 65.5 us -> 0.02 us
  blocking collectives: 138 us -> 73.5 us
  Pallas kernels: 0 us -> 19.9 us
  waiting for transfers between devices: 0 us -> 18 us
  starting transfers between devices: 0 us -> 15.9 us
  matrix products: 14.9 us -> 0 us
  other arithmetic: 9.34 us -> 0 us
    all_to_all x5 -> x2, blocking collectives: 138 us -> 73.5 us  [the longest x1 52.6 us: local(): lax.all_to_all(sending, LAT, split_axis=0, concat_axis=0, tiled=True)]
    all_to_all x3 -> x0, local copies, waits for them, and re-layouts: 30 us -> none  [the longest x2 29.8 us: local(): lax.all_to_all(sending, 'lat', split_axis=3, concat_axis=2, tiled=True)]
    unnamed x16 -> x10, local copies, waits for them, and re-layouts: 20.8 us -> 0.02 us
    pallas_call x0 -> x6, Pallas kernels: none -> 19.9 us  [the longest x1 7.63 us: spread_out(): pl.pallas_call(spread_out_kernel, grid_spec=pltpu.PrefetchScalarGridSpec(...]
    all_to_all x0 -> x1, waiting for transfers between devices: none -> 15.3 us  [local(): lax.all_to_all(chip.reshape(peers, each, *chip.shape[1:]), RING, split_ax...]
    dot_general x3 -> x0, matrix products: 14.9 us -> none  [the longest x1 7.3 us: local(): jnp.einsum('lj,mjab->mlab', vert_loc, along_lon, preferred_element_type=j...]
    convert_element_type x1 -> x0, local copies, waits for them, and re-layouts: 13 us -> none  [local(): sending = jnp.einsum('lj,mjab->mlab', vert_loc, along_lon, preferred_elem...]
    all_to_all x0 -> x1, starting transfers between devices: none -> 9.21 us  [local(): lax.all_to_all(chip.reshape(peers, each, *chip.shape[1:]), RING, split_ax...]
  transfers between devices with their start and end apart: 0 -> 3, of which waited for: 0 -> 3; matrix products, arithmetic and copies ran while one was open for 0% -> 0% of each run, Pallas kernels for 0% -> 0%
where the time goes in v1:
time: 128 us; the launch traced here: 127 us
  blocking collectives  73.5 us (57%)
  Pallas kernels  19.9 us (16%)
  waiting for transfers between devices  18 us (14%)
  starting transfers between devices  15.9 us (12%)
    all_to_all x1, blocking collectives, local(): lax.all_to_all(sending, LAT, split_axis=0, concat_axis=0, tiled=True)  52.6 us
    all_to_all x1, blocking collectives, local(): lax.all_to_all(copies, RING, split_axis=0, concat_axis=0, tiled=True)  20.9 us
    all_to_all x1, waiting for transfers between devices, local(): lax.all_to_all(chip.reshape(peers, each, *chip.shape[1:]), RING, split_ax...  15.3 us
    all_to_all x1, starting transfers between devices, local(): lax.all_to_all(chip.reshape(peers, each, *chip.shape[1:]), RING, split_ax...  9.21 us
    pallas_call x1, Pallas kernels, spread_out(): pl.pallas_call(spread_out_kernel, grid_spec=pltpu.PrefetchScalarGridSpec(...  7.63 us
    pallas_call x2, Pallas kernels, half_sum(): pl.pallas_call(half_sum_kernel, grid_spec=pltpu.PrefetchScalarGridSpec(nu...  7.47 us
    pallas_call x1, Pallas kernels, finish(): pl.pallas_call(finish_kernel, grid=(members,), in_specs=[pl.BlockSpec((LA...  3.65 us
    ppermute x1, starting transfers between devices, local(): other = lax.ppermute(own, 'core', swap)  3.38 us
  transfers between devices with their start and end apart: 3, of which 3 were waited for; matrix products, arithmetic and copies ran while one was open for 0% of the time, Pallas kernels for 0%

profile of v1, /device:TPU:1, one launch (start us, length us, event | category | flops | bytes accessed | tf_op | source)
XLA Modules:
  0.0 127.3 jit_solution(16884695334971588556)
XLA Ops:
  0.0 3.2 %half_sum.2 = bf16[32,32,256]{2,1,0:T(8,128)(2,1)S(1)} custom-call(s32[1]{0:T(128)} %bitcast.2.start_ref, bf16[4,64,32,256]{3,2,1,0:T(8,128)(2,1)} %spread_ref.5, bf16[4,64,32,256]{3,2,1,0:T(8,128)(2,1)} %controls_ref.3), custom_call_target="tpu_custom_call" | custom-call | tf_op jit(solution)/shard_map/half_sum/pallas_call | solution.py:47
  3.2 3.3 %collective-permute-start = (bf16[32,32,256]{2,1,0:T(8,128)(2,1)S(1)}, bf16[32,32,256]{2,1,0:T(8,128)(2,1)S(1)}, u32[]{:S(2)}, u32[]{:S(2)}) collective-permute-start(bf16[32,32,256]{2,1,0:T(8,128)(2,1)S(1)} %half_sum.2), channel_id=1, source_target_pairs={{0,8},{8,0},{1,9},{9,1},{2,10},{10,2},{3,11},{11,3},{4,12},{12,4},... | collective-permute-start | bytes 1572872 | tf_op jit(solution)/shard_map/ppermute | solution.py:232
  6.5 1.5 %collective-permute-done.rest_0_ = bf16[32,32,256]{2,1,0:T(8,128)(2,1)S(1)} collective-permute-done((bf16[32,32,256]{2,1,0:T(8,128)(2,1)S(1)}, bf16[32,32,256]{2,1,0:T(8,128)(2,1)S(1)}, u32[]{:S(2)}, u32[]{:S(2)}) %collective-permute-start) | collective-permute-done | bytes 524320 | tf_op jit(solution)/shard_map/ppermute | solution.py:232
  8.0 0.0 copy-start.2
  8.0 0.0 copy-start.4
  8.0 0.0 copy-start.1
  8.0 0.0 copy-start.3
  8.0 0.0 copy-start
  8.0 4.3 %half_sum.3 = bf16[32,32,256]{2,1,0:T(8,128)(2,1)} custom-call(s32[1]{0:T(128)} %bitcast.start_ref.half_ref, bf16[4,64,32,256]{3,2,1,0:T(8,128)(2,1)} %spread_ref.5, bf16[4,64,32,256]{3,2,1,0:T(8,128)(2,1)} %controls_ref.3, bf16[32,32,256]{2,1,0:T(8,128)(2,1)S(1)} %collective-permute-done.rest_0_), custom_call_target="tpu_custom_call" | custom-call | tf_op jit(solution)/shard_map/half_sum/pallas_call | solution.py:47
  12.3 9.2 %all-to-all-start = ((bf16[16,2,32,256]{3,2,1,0:T(8,128)(2,1)}), bf16[16,2,32,256]{3,2,1,0:T(8,128)(2,1)S(1)}, u32[]{:S(2)}, u32[]{:S(2)}) async-start(bf16[16,2,32,256]{3,2,1,0:T(8,128)(2,1)} %bitcast.3), calls=%async_computation | async-start | bytes 1048576 | tf_op jit(solution)/shard_map/all_to_all | solution.py:236
  21.6 15.3 %all-to-all-done.pieces_ref = bf16[16,2,32,256]{3,2,1,0:T(8,128)(2,1)S(1)} async-done(((bf16[16,2,32,256]{3,2,1,0:T(8,128)(2,1)}), bf16[16,2,32,256]{3,2,1,0:T(8,128)(2,1)S(1)}, u32[]{:S(2)}, u32[]{:S(2)}) %all-to-all-start) | async-done | bytes 524320 | tf_op jit(solution)/shard_map/all_to_all | solution.py:236
  36.9 0.0 copy-done.2
  36.9 0.0 copy-done.4
  36.9 0.7 weigh.1
  37.6 20.9 %all_to_all.15 = bf16[16,2,32,256]{3,2,1,0:T(8,128)(2,1)S(1)} all-to-all(bf16[16,2,32,256]{3,2,1,0:T(8,128)(2,1)S(1)} %weigh.1), channel_id=1, replica_groups=mesh['zh'=4,'y'=4,'core'=2,'lat'=8] {'zh','y'}, dimensions={0} | all-to-all | bytes 1048576 | tf_op jit(solution)/shard_map/all_to_all | solution.py:241
  58.5 3.4 %collective-permute-start.1 = (bf16[32,32,256]{2,1,0:T(8,128)(2,1)S(1)}, bf16[32,32,256]{2,1,0:T(8,128)(2,1)S(1)}, u32[]{:S(2)}, u32[]{:S(2)}) collective-permute-start(bf16[32,32,256]{2,1,0:T(8,128)(2,1)S(1)} %bitcast.6), channel_id=1, source_target_pairs={{0,8},{8,0},{1,9},{9,1},{2,10},{10,2},{3,11},{11,3},{4,12},{12,4},... | collective-permute-start | bytes 1572872 | tf_op jit(solution)/shard_map/ppermute | solution.py:242
  61.9 0.0 copy-done.1
  61.9 0.0 copy-done.3
  61.9 0.4 tables.1
  62.3 1.1 collective-permute-done.1.other_ref
  63.4 0.0 copy-done
  63.4 7.6 %spread_out.1 = bf16[8,4,32,2048]{3,2,1,0:T(8,128)(2,1)S(1)} custom-call(s32[1]{0:T(128)} %bitcast.start_ref.half_ref, bf16[4,64,32,256]{3,2,1,0:T(8,128)(2,1)} %spread_ref.5, bf16[32,32,256]{2,1,0:T(8,128)(2,1)S(1)} %bitcast.7, bf16[32,32,256]{2,1,0:T(8,128)(2,1)S(1)} %collective-permute-done.1.other_ref, bf16[512,512]{1,0:T(8,128)(2,1)S(1)} %get-tuple-element.7.big_ref, ...), custom_call_target="tpu_custom_call" | custom-call | tf_op jit(solution)/shard_map/spread_out/pallas_call | solution.py:129
  71.0 52.6 %all_to_all.16.parts_ref = bf16[8,4,32,2048]{3,2,1,0:T(8,128)(2,1)S(1)} all-to-all(bf16[8,4,32,2048]{3,2,1,0:T(8,128)(2,1)S(1)} %spread_out.1), channel_id=1, replica_groups=mesh['zh'=4,'y'=4,'core'=2,'lat'=8] {'lat'}, dimensions={0} | all-to-all | bytes 8388608 | tf_op jit(solution)/shard_map/all_to_all | solution.py:244
  123.7 3.6 %finish.1 = bf16[4,64,32,256]{3,2,1,0:T(8,128)(2,1)} custom-call(bf16[8,4,32,2048]{3,2,1,0:T(8,128)(2,1)S(1)} %all_to_all.16.parts_ref, bf16[4,256,256]{2,1,0:T(8,128)(2,1)S(1)} %get-tuple-element.8.turned_ref), custom_call_target="tpu_custom_call" | custom-call | tf_op jit(solution)/shard_map/finish/pallas_call | solution.py:179
Async XLA Ops:
  3.2 4.8 %collective-permute-start = (bf16[32,32,256]{2,1,0:T(8,128)(2,1)S(1)}, bf16[32,32,256]{2,1,0:T(8,128)(2,1)S(1)}, u32[]{:S(2)}, u32[]{:S(2)}) collective-permute-start(bf16[32,32,256]{2,1,0:T(8,128)(2,1)S(1)} %half_sum.2), channel_id=1, source_target_pairs={{0,8},{8,0},{1,9},{9,1},{2,10},{10,2},{3,11},{11,3},{4,12},{12,4},... | collective-permute-start | bytes 1572872 | tf_op jit(solution)/shard_map/ppermute | solution.py:232
  8.0 28.8 %copy-start.2 = (s32[32,256]{1,0:T(8,128)S(1)}, s32[32,256]{1,0:T(8,128)}, u32[]{:S(2)}) copy-start(s32[32,256]{1,0:T(8,128)} %classes_ref.1) | copy-start | bytes 98308
  8.0 28.8 %copy-start.4 = (f32[8,64]{1,0:T(8,128)S(1)}, f32[8,64]{1,0:T(8,128)}, u32[]{:S(2)}) copy-start(f32[8,64]{1,0:T(8,128)} %table_ref.1) | copy-start | bytes 6148
  8.0 53.9 %copy-start.1 = (bf16[256,256]{1,0:T(8,128)(2,1)S(1)}, bf16[256,256]{1,0:T(8,128)(2,1)}, u32[]{:S(2)}) copy-start(bf16[256,256]{1,0:T(8,128)(2,1)} %lat_ref.1) | copy-start | bytes 393220
  8.0 53.9 %copy-start.3 = (bf16[64,64]{1,0:T(8,128)(2,1)S(1)}, bf16[64,64]{1,0:T(8,128)(2,1)}, u32[]{:S(2)}) copy-start(bf16[64,64]{1,0:T(8,128)(2,1)} %vert_ref.1) | copy-start | bytes 24580
  8.0 55.4 %copy-start = (bf16[256,256]{1,0:T(8,128)(2,1)S(1)}, bf16[256,256]{1,0:T(8,128)(2,1)}, u32[]{:S(2)}) copy-start(bf16[256,256]{1,0:T(8,128)(2,1)} %lon_ref.1) | copy-start | bytes 393220
  12.3 24.5 %all-to-all-start = ((bf16[16,2,32,256]{3,2,1,0:T(8,128)(2,1)}), bf16[16,2,32,256]{3,2,1,0:T(8,128)(2,1)S(1)}, u32[]{:S(2)}, u32[]{:S(2)}) async-start(bf16[16,2,32,256]{3,2,1,0:T(8,128)(2,1)} %bitcast.3), calls=%async_computation | async-start | bytes 1048576 | tf_op jit(solution)/shard_map/all_to_all | solution.py:236
  58.5 4.9 %collective-permute-start.1 = (bf16[32,32,256]{2,1,0:T(8,128)(2,1)S(1)}, bf16[32,32,256]{2,1,0:T(8,128)(2,1)S(1)}, u32[]{:S(2)}, u32[]{:S(2)}) collective-permute-start(bf16[32,32,256]{2,1,0:T(8,128)(2,1)S(1)} %bitcast.6), channel_id=1, source_target_pairs={{0,8},{8,0},{1,9},{9,1},{2,10},{10,2},{3,11},{11,3},{4,12},{12,4},... | collective-permute-start | bytes 1572872 | tf_op jit(solution)/shard_map/ppermute | solution.py:242
